TPU v7x, 512 devices: a whole 4x8x8 slice. The times are simulated.
512 devices in a mesh: rows: 128 (over y, z, core), rank: 4 (over x).
Axes of the slice: x: 4, y: 8, z: 8, core: 2. Of those that a mesh axis runs over, the one named last changes fastest.
Arguments:
- left_factor: bfloat16 [128, 262144], P(None, 'rows'), may hold values from -8 to 8
- right_factor: bfloat16 [128, 262144], P(None, 'rows'), may hold values from -8 to 8
- left_plan: float32 [256, 262144], P('rank', 'rows'), may hold values from 0.0068 to 147, as said below
- right_plan: float32 [256, 262144], P('rank', 'rows'), may hold values from 0.0068 to 147, as said below
- log_inner: float32 [256], P('rank'), may hold values from -1 to 1
- left_mass: float32 [262144], P('rows'), may hold values from 32 to 1024, as said below
- right_mass: float32 [262144], P('rows'), may hold values from 32 to 1024, as said below
Outputs:
- new_left: float32 [256, 262144], P('rank', 'rows')
- new_right: float32 [256, 262144], P('rank', 'rows')
- new_log_inner: float32 [256], P('rank')
Inputs may be any that keep to these rules, and one draw needn't show every extreme that they name: `left_plan`: positive entries. `right_plan`: positive entries. `left_mass`: positive point masses. `right_mass`: positive point masses.
All inputs are finite; a program needn't handle non-finite values. Where the computation divides by a largest or mean magnitude, that divisor is 1e-20 or more.
Results may differ from a plain program's by a relative error of at most 0.00045.
Values sent between devices are 32-bit elements; how exact they have to be, the bound alone decides.
A program may use at most 64 MiB of HBM per device.

v0:
```python
import jax
import jax.numpy as jnp
from jax import lax
from jax.sharding import Mesh
from jax.sharding import PartitionSpec as P

RANK = 256
ITERS = 3
ROWS = ("rows_0", "rows_1", "rows_2")
ROWS_RANK = ("rows_0", "rows_1", "rows_2", "rank")


def by_axis(x, axes):
    for axis in axes:
        x = lax.psum(x, axis)
    return x


def by_axis_2(x, axes):
    for axis in axes:
        x = lax.pmax(x, axis)
    return x


def from_everyone(x, axis):
    copies = jnp.broadcast_to(x, (lax.axis_size(axis), *x.shape))
    return lax.all_to_all(copies, axis, split_axis=0, concat_axis=0, tiled=True)


def of_everyone(x, axis):
    return from_everyone(x, axis).sum(axis=0)


def in_one(arrays, axis):
    ravelled, at, outs = (jnp.concatenate([a.reshape(-1) for a in arrays]), 0, [])
    subtotal = of_everyone(ravelled, axis)
    for a in arrays:
        outs.append(subtotal[at : at + a.size].reshape(a.shape))
        at += a.size
    return tuple(outs)


def contract_points(factor, plan):
    return lax.dot_general(
        factor, plan, (((1,), (1,)), ((), ())), preferred_element_type=jnp.float32
    )


def expand_points(projected, factor):
    return lax.dot_general(
        projected, factor, (((0,), (0,)), ((), ())), preferred_element_type=jnp.float32
    )


def balance(inner_mass, col_scale_left, col_total_left, col_scale_right, col_total_right):
    mixed = (
        jnp.log(inner_mass)
        + jnp.log(col_scale_left * col_total_left)
        + jnp.log(col_scale_right * col_total_right)
    )
    inner_mass = jnp.exp(mixed / 3.0)
    return (inner_mass, inner_mass / col_total_left, inner_mass / col_total_right)


def per_device(left_factor, right_factor, left_plan, right_plan, log_inner, left_mass, right_mass):
    precise = lax.Precision.HIGHEST
    columns = left_plan.shape[0]
    left_round = left_plan.astype(jnp.bfloat16)
    right_round = right_plan.astype(jnp.bfloat16)
    proj_right, proj_left, total_left, total_right = (
        by_axis(contract_points(right_factor, right_round), ROWS),
        by_axis(contract_points(left_factor, left_round), ROWS),
        by_axis(jnp.sum(left_mass), ROWS),
        by_axis(jnp.sum(right_mass), ROWS),
    )
    inner_mass = total_left / RANK * jnp.exp(log_inner)
    scaled_right = (proj_right / inner_mass[None, :]).astype(jnp.bfloat16)
    scaled_left = (proj_left / inner_mass[None, :]).astype(jnp.bfloat16)
    grad_left = expand_points(scaled_right, left_factor)
    grad_right = expand_points(scaled_left, right_factor)
    pairing = jnp.sum(scaled_right.astype(jnp.float32) * proj_left, axis=0)
    grad_inner = -pairing / inner_mass
    local_top = jnp.maximum(
        jnp.maximum(jnp.max(jnp.abs(grad_left)), jnp.max(jnp.abs(grad_right))),
        jnp.max(jnp.abs(grad_inner)),
    )
    largest = by_axis_2(local_top, ROWS_RANK)
    step_size = 5.0 / jnp.maximum(largest, 0.25)
    tilted_left = left_plan * jnp.exp(-step_size * grad_left)
    tilted_right = right_plan * jnp.exp(-step_size * grad_right)
    inner_mass = inner_mass * jnp.exp(-step_size * grad_inner)
    right_norm = right_mass * (total_left / total_right)
    row_scale_left = left_mass
    row_scale_right = right_norm
    own_left = jnp.ones((columns,), jnp.float32)
    own_right = jnp.ones((columns,), jnp.float32)
    own_inner = inner_mass
    for repeat in range(ITERS):
        rows_left, rows_right = in_one(
            (
                jnp.dot(own_left, tilted_left, precision=precise),
                jnp.dot(own_right, tilted_right, precision=precise),
            ),
            "rank",
        )
        row_scale_left = left_mass / rows_left
        row_scale_right = right_norm / rows_right
        col_total_left, col_total_right = (
            by_axis(jnp.dot(tilted_left, row_scale_left, precision=precise), ROWS),
            by_axis(jnp.dot(tilted_right, row_scale_right, precision=precise), ROWS),
        )
        own_inner, own_left, own_right = balance(
            own_inner, own_left, col_total_left, own_right, col_total_right
        )
    new_left = row_scale_left[None, :] * tilted_left * own_left[:, None]
    new_right = row_scale_right[None, :] * tilted_right * own_right[:, None]
    new_log_inner = jnp.log(own_inner) - jnp.log(total_left / RANK)
    return (new_left, new_right, new_log_inner)


def solution(mesh):
    split = Mesh(
        mesh.devices.reshape(8, 8, 2, mesh.shape["rank"]), ("rows_0", "rows_1", "rows_2", "rank")
    )
    placed = (
        P(None, ROWS),
        P(None, ROWS),
        P("rank", ROWS),
        P("rank", ROWS),
        P("rank"),
        P(ROWS),
        P(ROWS),
    )
    return jax.shard_map(
        per_device,
        mesh=split,
        in_specs=placed,
        out_specs=(P("rank", ROWS), P("rank", ROWS), P("rank")),
        check_vma=False,
    )
```

profile of v0, /device:TPU:1, one launch (start us, length us, event | category | flops | bytes accessed | tf_op | source)
XLA Modules:
  0.0 266.5 jit_solution(6628564272634690493)
XLA Ops:
  0.7 1.4 reduce_sum.57
  2.6 1.4 fusion
  4.4 26.2 %all-reduce.15 = (f32[128,64]{0,1:T(8,128)S(1)}, f32[]{:T(128)}, f32[128,64]{0,1:T(8,128)S(1)}, f32[]{:T(128)}) all-reduce(f32[128,64]{0,1:T(8,128)S(1)} %fusion.2, f32[]{:T(128)} %reduce_sum.54, f32[128,64]{0,1:T(8,128)S(1)} %fusion, f32[]{:T(128)} %reduce_sum.57), channel_id=1, replica_groups=mesh['rows_0'=8,'rows_1'=8,'rows_2'=2,'rank'=4] {'rows_0'}, use_global_device_ids=true, to_apply=%region_4.0 | all-reduce | flops 16386 | bytes 131088 | tf_op jit(solution)/shard_map/psum | solution.py:15
  30.6 30.3 %all-reduce.16 = (f32[128,64]{0,1:T(8,128)S(1)}, f32[]{:T(128)}, f32[128,64]{0,1:T(8,128)S(1)}, f32[]{:T(128)}) all-reduce(f32[128,64]{0,1:T(8,128)S(1)} %get-tuple-element.19, f32[]{:T(128)} %get-tuple-element.20, f32[128,64]{0,1:T(8,128)S(1)} %get-tuple-element.21, ...), channel_id=1, replica_groups=mesh['rows_0'=8,'rows_1'=8,'rows_2'=2,'rank'=4] {'rows_1'}, use_global_device_ids=true, to_apply=%region_5.0 | all-reduce | flops 16386 | bytes 131088 | tf_op jit(solution)/shard_map/psum | solution.py:15
  60.9 19.6 %all-reduce.17 = (f32[128,64]{0,1:T(8,128)S(1)}, f32[]{:T(128)}, f32[128,64]{0,1:T(8,128)S(1)}, f32[]{:T(128)}) all-reduce(f32[128,64]{0,1:T(8,128)S(1)} %get-tuple-element.9, f32[]{:T(128)} %get-tuple-element.10, f32[128,64]{0,1:T(8,128)S(1)} %get-tuple-element.11, ...), channel_id=1, replica_groups=mesh['rows_0'=8,'rows_1'=8,'rows_2'=2,'rank'=4] {'rows_2'}, use_global_device_ids=true, to_apply=%region_6.0 | all-reduce | flops 16386 | bytes 131088 | tf_op jit(solution)/shard_map/psum | solution.py:15
  85.7 11.2 %pmax.28 = f32[]{:T(128)} all-reduce(f32[]{:T(128)S(6)} %max.18), channel_id=1, replica_groups=mesh['rows_0'=8,'rows_1'=8,'rows_2'=2,'rank'=4] {'rows_0'}, use_global_device_ids=true, to_apply=%region_14.0 | all-reduce | flops 1 | bytes 8 | tf_op jit(solution)/shard_map/pmax | solution.py:21
  96.9 11.3 %pmax.29 = f32[]{:T(128)} all-reduce(f32[]{:T(128)} %pmax.28), channel_id=1, replica_groups=mesh['rows_0'=8,'rows_1'=8,'rows_2'=2,'rank'=4] {'rows_1'}, use_global_device_ids=true, to_apply=%region_15.0 | all-reduce | flops 1 | bytes 8 | tf_op jit(solution)/shard_map/pmax | solution.py:21
  108.2 9.9 %pmax.30 = f32[]{:T(128)} all-reduce(f32[]{:T(128)} %pmax.29), channel_id=1, replica_groups=mesh['rows_0'=8,'rows_1'=8,'rows_2'=2,'rank'=4] {'rows_2'}, use_global_device_ids=true, to_apply=%region_16.0 | all-reduce | flops 1 | bytes 8 | tf_op jit(solution)/shard_map/pmax | solution.py:21
  118.1 9.1 %pmax.31 = f32[]{:T(128)} all-reduce(f32[]{:T(128)} %pmax.30), channel_id=1, replica_groups=mesh['rows_0'=8,'rows_1'=8,'rows_2'=2,'rank'=4] {'rank'}, use_global_device_ids=true, to_apply=%region_17.0 | all-reduce | flops 1 | bytes 8 | tf_op jit(solution)/shard_map/pmax | solution.py:21
  127.9 1.2 exponential_multiply_fusion
  130.5 3.3 %all-to-all-start = ((f32[4,1,4096]{2,1,0:T(1,128)}), f32[4,1,4096]{2,1,0:T(1,128)S(1)}, u32[]{:S(2)}, u32[]{:S(2)}) async-start(f32[4,1,4096]{2,1,0:T(1,128)} %broadcast_in_dim.6), calls=%async_computation | async-start | bytes 131072 | tf_op jit(solution)/shard_map/all_to_all | solution.py:27
  135.1 3.1 %all-to-all-done = f32[4,1,4096]{2,1,0:T(1,128)S(1)} async-done(((f32[4,1,4096]{2,1,0:T(1,128)}), f32[4,1,4096]{2,1,0:T(1,128)S(1)}, u32[]{:S(2)}, u32[]{:S(2)}) %all-to-all-start) | async-done | bytes 65568 | tf_op jit(solution)/shard_map/all_to_all | solution.py:27
  139.3 12.4 %all-reduce.6 = (f32[64]{0:T(128)S(1)}, f32[64]{0:T(128)S(1)}) all-reduce(f32[64]{0:T(128)S(1)} %convolution_bitcast_fusion.4, f32[64]{0:T(128)S(1)} %convolution_bitcast_fusion.5), channel_id=1, replica_groups=mesh['rows_0'=8,'rows_1'=8,'rows_2'=2,'rank'=4] {'rows_0'}, use_global_device_ids=true, to_apply=%region_26.0 | all-reduce | flops 128 | bytes 1024 | tf_op jit(solution)/shard_map/psum | solution.py:15
  151.7 12.4 %all-reduce.2 = (f32[64]{0:T(128)S(1)}, f32[64]{0:T(128)S(1)}) all-reduce(f32[64]{0:T(128)S(1)} %get-tuple-element.17, f32[64]{0:T(128)S(1)} %get-tuple-element.18), channel_id=1, replica_groups=mesh['rows_0'=8,'rows_1'=8,'rows_2'=2,'rank'=4] {'rows_1'}, use_global_device_ids=true, to_apply=%region_27.0 | all-reduce | flops 128 | bytes 1024 | tf_op jit(solution)/shard_map/psum | solution.py:15
  164.1 13.1 %all-reduce.10 = (f32[64]{0:T(128)S(1)}, f32[64]{0:T(128)S(1)}) all-reduce(f32[64]{0:T(128)S(1)} %get-tuple-element.7, f32[64]{0:T(128)S(1)} %get-tuple-element.8), channel_id=1, replica_groups=mesh['rows_0'=8,'rows_1'=8,'rows_2'=2,'rank'=4] {'rows_2'}, use_global_device_ids=true, to_apply=%region_28.0 | all-reduce | flops 128 | bytes 1024 | tf_op jit(solution)/shard_map/psum | solution.py:15
  178.1 6.8 %all_to_all.18 = f32[4,1,4096]{2,1,0:T(1,128)S(1)} all-to-all(f32[4,1,4096]{2,1,0:T(1,128)S(1)} %broadcast_in_dim.7), channel_id=1, replica_groups=mesh['rows_0'=8,'rows_1'=8,'rows_2'=2,'rank'=4] {'rank'}, dimensions={0} | all-to-all | bytes 131072 | tf_op jit(solution)/shard_map/all_to_all | solution.py:27
  186.0 10.7 %all-reduce.5 = (f32[64]{0:T(128)S(1)}, f32[64]{0:T(128)S(1)}) all-reduce(f32[64]{0:T(128)S(1)} %convolution_bitcast_fusion.2, f32[64]{0:T(128)S(1)} %convolution_bitcast_fusion.3), channel_id=1, replica_groups=mesh['rows_0'=8,'rows_1'=8,'rows_2'=2,'rank'=4] {'rows_0'}, use_global_device_ids=true, to_apply=%region_33.0 | all-reduce | flops 128 | bytes 1024 | tf_op jit(solution)/shard_map/psum | solution.py:15
  196.7 10.7 %all-reduce.1 = (f32[64]{0:T(128)S(1)}, f32[64]{0:T(128)S(1)}) all-reduce(f32[64]{0:T(128)S(1)} %get-tuple-element.15, f32[64]{0:T(128)S(1)} %get-tuple-element.16), channel_id=1, replica_groups=mesh['rows_0'=8,'rows_1'=8,'rows_2'=2,'rank'=4] {'rows_1'}, use_global_device_ids=true, to_apply=%region_34.0 | all-reduce | flops 128 | bytes 1024 | tf_op jit(solution)/shard_map/psum | solution.py:15
  207.4 10.5 %all-reduce.9 = (f32[64]{0:T(128)S(1)}, f32[64]{0:T(128)S(1)}) all-reduce(f32[64]{0:T(128)S(1)} %get-tuple-element.5, f32[64]{0:T(128)S(1)} %get-tuple-element.6), channel_id=1, replica_groups=mesh['rows_0'=8,'rows_1'=8,'rows_2'=2,'rank'=4] {'rows_2'}, use_global_device_ids=true, to_apply=%region_35.0 | all-reduce | flops 128 | bytes 1024 | tf_op jit(solution)/shard_map/psum | solution.py:15
  219.4 3.3 %all-to-all-start.2 = ((f32[4,1,4096]{2,1,0:T(1,128)}), f32[4,1,4096]{2,1,0:T(1,128)S(1)}, u32[]{:S(2)}, u32[]{:S(2)}) async-start(f32[4,1,4096]{2,1,0:T(1,128)} %broadcast_in_dim.8), calls=%async_computation.2 | async-start | bytes 131072 | tf_op jit(solution)/shard_map/all_to_all | solution.py:27
  222.7 4.4 %all-to-all-done.2 = f32[4,1,4096]{2,1,0:T(1,128)S(1)} async-done(((f32[4,1,4096]{2,1,0:T(1,128)}), f32[4,1,4096]{2,1,0:T(1,128)S(1)}, u32[]{:S(2)}, u32[]{:S(2)}) %all-to-all-start.2) | async-done | bytes 65568 | tf_op jit(solution)/shard_map/all_to_all | solution.py:27
  228.2 12.4 %all-reduce.4 = (f32[64]{0:T(128)S(1)}, f32[64]{0:T(128)S(1)}) all-reduce(f32[64]{0:T(128)S(1)} %convolution_bitcast_fusion, f32[64]{0:T(128)S(1)} %convolution_bitcast_fusion.1), channel_id=1, replica_groups=mesh['rows_0'=8,'rows_1'=8,'rows_2'=2,'rank'=4] {'rows_0'}, use_global_device_ids=true, to_apply=%region_40.0 | all-reduce | flops 128 | bytes 1024 | tf_op jit(solution)/shard_map/psum | solution.py:15
  240.6 12.4 %all-reduce = (f32[64]{0:T(128)S(1)}, f32[64]{0:T(128)S(1)}) all-reduce(f32[64]{0:T(128)S(1)} %get-tuple-element.13, f32[64]{0:T(128)S(1)} %get-tuple-element.14), channel_id=1, replica_groups=mesh['rows_0'=8,'rows_1'=8,'rows_2'=2,'rank'=4] {'rows_1'}, use_global_device_ids=true, to_apply=%region_41.0 | all-reduce | flops 128 | bytes 1024 | tf_op jit(solution)/shard_map/psum | solution.py:15
  253.0 11.1 %all-reduce.8 = (f32[64]{0:T(128)S(1)}, f32[64]{0:T(128)S(1)}) all-reduce(f32[64]{0:T(128)S(1)} %get-tuple-element.3, f32[64]{0:T(128)S(1)} %get-tuple-element.4), channel_id=1, replica_groups=mesh['rows_0'=8,'rows_1'=8,'rows_2'=2,'rank'=4] {'rows_2'}, use_global_device_ids=true, to_apply=%region_42.0 | all-reduce | flops 128 | bytes 1024 | tf_op jit(solution)/shard_map/psum | solution.py:15
  (51 shorter events, 12.9 us)
Async XLA Ops:
  0.6 2.0 copy-start
  0.6 1.4 copy-start.3
  2.6 1.4 copy-start.1
  2.6 1.4 copy-start.2
  80.4 0.7 copy-start.5
  130.5 7.7 %all-to-all-start = ((f32[4,1,4096]{2,1,0:T(1,128)}), f32[4,1,4096]{2,1,0:T(1,128)S(1)}, u32[]{:S(2)}, u32[]{:S(2)}) async-start(f32[4,1,4096]{2,1,0:T(1,128)} %broadcast_in_dim.6), calls=%async_computation | async-start | bytes 131072 | tf_op jit(solution)/shard_map/all_to_all | solution.py:27
  135.1 3.2 %copy-start.4 = (f32[2048]{0:T(1024)S(1)}, f32[2048]{0:T(1024)}, u32[]{:S(2)}) copy-start(f32[2048]{0:T(1024)} %param.13) | copy-start | bytes 24580
  219.4 7.7 %all-to-all-start.2 = ((f32[4,1,4096]{2,1,0:T(1,128)}), f32[4,1,4096]{2,1,0:T(1,128)S(1)}, u32[]{:S(2)}, u32[]{:S(2)}) async-start(f32[4,1,4096]{2,1,0:T(1,128)} %broadcast_in_dim.8), calls=%async_computation.2 | async-start | bytes 131072 | tf_op jit(solution)/shard_map/all_to_all | solution.py:27
where the time goes:
time: 267 us; the launch traced here: 266 us
  blocking collectives  230 us (86%)
  matrix products  8.87 us (3%)
  waiting for transfers between devices  7.49 us (3%)
  other arithmetic  6.57 us (2%)
  starting transfers between devices  6.57 us (2%)
  between operations  5.45 us (2%)
    psum x12, blocking collectives, by_axis(): x = lax.psum(x, axis)  182 us
    pmax x4, blocking collectives, by_axis_2(): x = lax.pmax(x, axis)  41.5 us
    all_to_all x2, waiting for transfers between devices, from_everyone(): return lax.all_to_all(copies, axis, split_axis=0, concat_axis=0, tiled=True)  7.49 us
    all_to_all x1, blocking collectives, from_everyone(): return lax.all_to_all(copies, axis, split_axis=0, concat_axis=0, tiled=True)  6.84 us
    all_to_all x2, starting transfers between devices, from_everyone(): return lax.all_to_all(copies, axis, split_axis=0, concat_axis=0, tiled=True)  6.57 us
  transfers between devices with their start and end apart: 2, of which 2 were waited for; matrix products, arithmetic and copies ran while one was open for 0% of the time, Pallas kernels for 0%

commit v1 on v0

v1 whole, which is shorter than its diff:
```python
import functools

import jax
import jax.numpy as jnp
from jax import lax
from jax.experimental import pallas as pl
from jax.experimental.pallas import tpu as pltpu
from jax.sharding import Mesh
from jax.sharding import PartitionSpec as P

ITERS = 3
LANES = 128
ROWS = ("y", "z", "c")
F32 = jnp.float32


def far_first(size):
    return sorted(range(1, size), key=lambda d: -min(d, size - d))


def kernel(
    sizes,
    lf_hbm,
    rf_hbm,
    lp_hbm,
    rp_hbm,
    li_ref,
    lm_ref,
    rm_ref,
    ol_hbm,
    or_hbm,
    oi_ref,
    lf,
    rf,
    plan,
    grad,
    src,
    r1,
    r2,
    full,
    m1,
    m2,
    rx,
    rs,
    c1,
    c2,
    load_sem,
    store_sem,
    send_sem,
    recv_sem,
):
    ny, nz, nc, nx = sizes
    half = LANES // 2
    points = lf.shape[1]
    tiles = points // LANES
    rank = half * nx
    y, z, c, x = (lax.axis_index(a) for a in ("y", "z", "c", "x"))
    yc_size, zx_size = ny * nc, nz * nx
    yc, zx = y * nc + c, z * nx + x
    piece = LANES // yc_size

    yc_peers = [
        {"y": lax.rem(y + dy, ny), "c": lax.rem(c + dc, nc)}
        for dy in far_first(ny) + [0]
        for dc in range(nc)
        if dy or dc
    ]
    z_peers = [{"z": lax.rem(z + dz, nz)} for dz in far_first(nz)]
    x_peers = [{"x": lax.rem(x + dx, nx)} for dx in far_first(nx)]
    zx_peers = [
        {"z": lax.rem(z + dz, nz), "x": lax.rem(x + dx, nx)}
        for dz in far_first(nz) + [0]
        for dx in far_first(nx) + [0]
        if dz or dx
    ]

    loads = [
        pltpu.make_async_copy(a, b, load_sem.at[i])
        for i, (a, b) in enumerate(
            (
                (rp_hbm, plan.at[half:]),
                (rf_hbm, rf),
                (lp_hbm, plan.at[:half]),
                (lf_hbm, lf),
            )
        )
    ]
    for load in loads:
        load.start()
    barrier = pltpu.get_barrier_semaphore()
    greeted = zx_peers + yc_peers
    for peer in greeted:
        pl.semaphore_signal(
            barrier, inc=1, device_id=peer, device_id_type=pl.DeviceIdType.MESH
        )

    def send(stage, source, target, peer):
        pltpu.make_async_remote_copy(
            src_ref=source,
            dst_ref=target,
            send_sem=send_sem.at[stage],
            recv_sem=recv_sem.at[stage],
            device_id=peer,
            device_id_type=pl.DeviceIdType.MESH,
        ).start()

    sent = []

    def spread(stage, ref, peers):
        for peer in peers:
            send(stage, ref, ref, peer)

    def arrived(stage, bulk):
        pltpu.make_async_copy(bulk, bulk, recv_sem.at[stage]).wait()
        sent.append((stage, bulk))

    lane = lax.broadcasted_iota(jnp.int32, (1, LANES), 1)
    low = lane < half
    eye = lax.broadcasted_iota(jnp.int32, (LANES, LANES), 0) == lax.broadcasted_iota(
        jnp.int32, (LANES, LANES), 1
    )

    def to_column(row):
        return jnp.sum(jnp.where(eye, row, 0.0), axis=1, keepdims=True)

    def to_row(column):
        return jnp.sum(jnp.where(eye, column, 0.0), axis=0, keepdims=True)

    def swap(row):
        return jnp.concatenate([row[:, half:], row[:, :half]], axis=1)

    def product(rows, factor):
        return lax.dot_general(
            plan[rows, :].astype(jnp.bfloat16),
            factor[...],
            (((1,), (1,)), ((), ())),
            preferred_element_type=F32,
        )

    lower, upper = slice(0, half), slice(half, LANES)
    mass_left = jnp.sum(lm_ref[...], axis=0, keepdims=True)
    mass_right = jnp.sum(rm_ref[...], axis=0, keepdims=True)
    masses = jnp.where(low, mass_left + swap(mass_left), mass_right + swap(mass_right))
    loads[0].wait()
    loads[1].wait()
    per = half // piece
    src[0:per, 0:piece, :] = product(upper, rf).reshape(per, piece, LANES)
    loads[2].wait()
    loads[3].wait()
    src[per : 2 * per, 0:piece, :] = product(lower, lf).reshape(per, piece, LANES)
    src[:, piece : piece + 1, :] = jnp.broadcast_to(
        masses.reshape(1, 1, LANES), (yc_size, 1, LANES)
    )
    pl.semaphore_wait(barrier, len(greeted))

    for peer in yc_peers:
        send(0, src.at[peer["y"] * nc + peer["c"]], r1.at[yc], peer)
    r1[yc] = src[yc]
    log_inner = jnp.concatenate([li_ref[...], li_ref[...]], axis=1)
    inner_base = jnp.exp(to_column(log_inner))
    arrived(0, r1.at[pl.ds(0, yc_size - 1)])
    r2[z] = jnp.sum(r1[...], axis=0)
    spread(1, r2.at[z], z_peers)
    arrived(1, r2.at[pl.ds(0, nz - 1)])
    summed = jnp.sum(r2[...], axis=0)
    mine = full.at[pl.ds(pl.multiple_of(yc * piece, piece), piece)]
    mine[...] = summed[:piece]
    spread(2, mine, yc_peers)
    masses = summed[piece:]
    total_left = jnp.sum(jnp.where(low, masses, 0.0), axis=1, keepdims=True)
    total_right = jnp.sum(jnp.where(low, 0.0, masses), axis=1, keepdims=True)
    mean_left = total_left / rank
    inner = mean_left * inner_base
    log_inner = jnp.log(mean_left) + log_inner
    right_norm = rm_ref[...] * (total_left / total_right)
    arrived(2, full.at[pl.ds(0, (yc_size - 1) * piece)])

    scaled = (full[...] / inner).astype(jnp.bfloat16)
    pairing = jnp.sum(
        scaled[lower].astype(F32) * full[upper, :], axis=1, keepdims=True
    )
    grad_inner = -pairing / inner[lower]
    grad_inner = to_row(jnp.concatenate([grad_inner, grad_inner], axis=0))

    width = 512 if points % 512 == 0 else LANES
    top = jnp.zeros((half, LANES), F32)
    for rows, factor in ((lower, lf), (upper, rf)):
        for at in range(0, points, width):
            part = jnp.dot(
                scaled[rows], factor[:, at : at + width], preferred_element_type=F32
            )
            grad[rows, at : at + width] = part
            part = jnp.abs(part)
            for k in range(0, width, LANES):
                top = jnp.maximum(top, part[:, k : k + LANES])
    top = jnp.maximum(jnp.max(top, axis=0, keepdims=True), jnp.abs(grad_inner))

    m1[yc] = top
    spread(3, m1.at[yc], yc_peers)
    arrived(3, m1.at[pl.ds(0, yc_size - 1)])
    m2[zx] = jnp.max(m1[...], axis=0)
    spread(4, m2.at[zx], zx_peers)
    arrived(4, m2.at[pl.ds(0, zx_size - 1)])
    largest = jnp.max(jnp.max(m2[...], axis=0), axis=1, keepdims=True)
    step = 5.0 / jnp.maximum(largest, 0.25)

    sides = ((0, lower, lm_ref[...]), (1, upper, right_norm))
    log_inner = log_inner - step * grad_inner
    scale_row = jnp.ones((1, LANES), F32)
    scale = None
    stage = 5
    for turn in range(ITERS):
        for side, rows, _ in sides:
            for t in range(tiles):
                at = slice(t * LANES, (t + 1) * LANES)
                if turn == 0:
                    tilted = plan[rows, at] * jnp.exp(-step * grad[rows, at])
                    plan[rows, at] = tilted
                else:
                    tilted = plan[rows, at] * scale[rows]
                rx[turn, side, x, t : t + 1, :] = jnp.sum(tilted, axis=0, keepdims=True)
            spread(stage + side, rx.at[turn, side, x], x_peers)
        sums = []
        for side, rows, mass in sides:
            arrived(stage + side, rx.at[turn, side, pl.ds(0, nx - 1)])
            rs[side] = mass / jnp.sum(rx[turn, side], axis=0)
            acc = jnp.zeros((half, LANES), F32)
            for t in range(tiles):
                acc += plan[rows, t * LANES : (t + 1) * LANES] * rs[side, t : t + 1, :]
            sums.append(jnp.sum(acc, axis=1, keepdims=True))
        c1[turn, yc] = to_row(jnp.concatenate(sums, axis=0))
        spread(stage + 2, c1.at[turn, yc], yc_peers)
        arrived(stage + 2, c1.at[turn, pl.ds(0, yc_size - 1)])
        c2[turn, z] = jnp.sum(c1[turn], axis=0)
        spread(stage + 3, c2.at[turn, z], z_peers)
        arrived(stage + 3, c2.at[turn, pl.ds(0, nz - 1)])
        totals = jnp.sum(c2[turn], axis=0)
        mixed = jnp.log(scale_row * totals)
        log_inner = (log_inner + (mixed + swap(mixed))) / 3.0
        scale_row = jnp.exp(log_inner) / totals
        scale = to_column(scale_row)
        stage += 4

    oi_ref[...] = (log_inner - jnp.log(mean_left))[:, :half]
    stores = []
    for side, rows, _ in sides:
        for t in range(tiles):
            at = slice(t * LANES, (t + 1) * LANES)
            grad[rows, at] = rs[side, t : t + 1, :] * plan[rows, at] * scale[rows]
        store = pltpu.make_async_copy(
            grad.at[rows], (ol_hbm, or_hbm)[side], store_sem.at[side]
        )
        store.start()
        stores.append(store)
    for number, bulk in sent:
        pltpu.make_async_copy(bulk, bulk, send_sem.at[number]).wait()
    for store in stores:
        store.wait()


def per_device(
    sizes, left_factor, right_factor, left_plan, right_plan, log_inner, left_mass, right_mass
):
    ny, nz, nc, nx = sizes
    depth, points = left_factor.shape
    columns = left_plan.shape[0]
    tiles = points // LANES
    yc_size, zx_size = ny * nc, nz * nx
    piece = LANES // yc_size
    stages = 5 + 4 * ITERS
    hbm = pl.BlockSpec(memory_space=pl.ANY)
    vmem = pl.BlockSpec(memory_space=pltpu.VMEM)
    new_left, new_right, new_log_inner = pl.pallas_call(
        functools.partial(kernel, sizes),
        out_shape=(
            jax.ShapeDtypeStruct((columns, points), F32),
            jax.ShapeDtypeStruct((columns, points), F32),
            jax.ShapeDtypeStruct((1, columns), F32),
        ),
        in_specs=[hbm] * 4 + [vmem] * 3,
        out_specs=(hbm, hbm, vmem),
        scratch_shapes=[
            pltpu.VMEM((depth, points), jnp.bfloat16),
            pltpu.VMEM((depth, points), jnp.bfloat16),
            pltpu.VMEM((2 * columns, points), F32),
            pltpu.VMEM((2 * columns, points), F32),
            pltpu.VMEM((yc_size, piece + 1, LANES), F32),
            pltpu.VMEM((yc_size, piece + 1, LANES), F32),
            pltpu.VMEM((nz, piece + 1, LANES), F32),
            pltpu.VMEM((LANES, LANES), F32),
            pltpu.VMEM((yc_size, 1, LANES), F32),
            pltpu.VMEM((zx_size, 1, LANES), F32),
            pltpu.VMEM((ITERS, 2, nx, tiles, LANES), F32),
            pltpu.VMEM((2, tiles, LANES), F32),
            pltpu.VMEM((ITERS, yc_size, 1, LANES), F32),
            pltpu.VMEM((ITERS, nz, 1, LANES), F32),
            pltpu.SemaphoreType.DMA((4,)),
            pltpu.SemaphoreType.DMA((2,)),
            pltpu.SemaphoreType.DMA((stages,)),
            pltpu.SemaphoreType.DMA((stages,)),
        ],
        compiler_params=pltpu.CompilerParams(collective_id=0, has_side_effects=True),
    )(
        left_factor,
        right_factor,
        left_plan,
        right_plan,
        log_inner.reshape(1, columns),
        left_mass.reshape(tiles, LANES),
        right_mass.reshape(tiles, LANES),
    )
    return new_left, new_right, new_log_inner.reshape(columns)


def solution(mesh):
    nx = mesh.shape["rank"]
    nc = 2
    ny = 1
    while mesh.shape["rows"] // nc > ny * ny:
        ny *= 2
    nz = mesh.shape["rows"] // (nc * ny)
    split = Mesh(mesh.devices.reshape(ny, nz, nc, nx), ("y", "z", "c", "x"))
    placed = (
        P(None, ROWS),
        P(None, ROWS),
        P("x", ROWS),
        P("x", ROWS),
        P("x"),
        P(ROWS),
        P(ROWS),
    )
    return jax.shard_map(
        functools.partial(per_device, (ny, nz, nc, nx)),
        mesh=split,
        in_specs=placed,
        out_specs=(P("x", ROWS), P("x", ROWS), P("x")),
        check_vma=False,
    )
```

time: 267 us -> 84.6 us (0.32)
  blocking collectives: 230 us -> 0 us
  Pallas kernels: 0 us -> 80.5 us
  matrix products: 8.87 us -> 0 us
  waiting for transfers between devices: 7.49 us -> 0 us
  other arithmetic: 6.57 us -> 0 us
  starting transfers between devices: 6.57 us -> 0 us
  between operations: 5.45 us -> 0.65 us
    psum x12 -> x0, blocking collectives: 182 us -> none  [by_axis(): x = lax.psum(x, axis)]
    pallas_call x0 -> x1, Pallas kernels: none -> 80.5 us  [per_device(): pl.pallas_call(functools.partial(kernel, sizes), out_shape=(jax.ShapeDtyp...]
    pmax x4 -> x0, blocking collectives: 41.5 us -> none  [by_axis_2(): x = lax.pmax(x, axis)]
    dot_general x16 -> x0, matrix products: 8.87 us -> none  [the longest x2 1.85 us: expand_points(): lax.dot_general(projected, factor, (((0,), (0,)), ((), ())), preferred_el...]
    all_to_all x2 -> x0, waiting for transfers between devices: 7.49 us -> none  [from_everyone(): return lax.all_to_all(copies, axis, split_axis=0, concat_axis=0, tiled=True)]
    all_to_all x1 -> x0, blocking collectives: 6.84 us -> none  [from_everyone(): return lax.all_to_all(copies, axis, split_axis=0, concat_axis=0, tiled=True)]
    all_to_all x2 -> x0, starting transfers between devices: 6.57 us -> none  [from_everyone(): return lax.all_to_all(copies, axis, split_axis=0, concat_axis=0, tiled=True)]
    unnamed x12 -> x7, local copies, waits for them, and re-layouts: 0.03 us -> 3.24 us
  transfers between devices with their start and end apart: 2 -> 0, of which waited for: 2 -> 0; matrix products, arithmetic and copies ran while one was open for 0% -> 0% of each run, Pallas kernels for 0% -> 0%
where the time goes in v1:
time: 84.6 us; the launch traced here: 84.4 us
  Pallas kernels  80.5 us (95%)
  local copies, waits for them, and re-layouts  3.24 us (4%)
    pallas_call x1, Pallas kernels, per_device(): pl.pallas_call(functools.partial(kernel, sizes), out_shape=(jax.ShapeDtyp...  80.5 us
    unnamed x7, local copies, waits for them, and re-layouts  3.24 us

profile of v1, /device:TPU:1, one launch (start us, length us, event | category | flops | bytes accessed | tf_op | source)
XLA Modules:
  0.0 84.4 jit_solution(5597036202377160107)
XLA Ops:
  0.6 80.5 %shard_map.94 = (f32[64,2048]{1,0:T(8,128)}, f32[64,2048]{1,0:T(8,128)}, f32[1,64]{1,0:T(1,128)}) custom-call(bf16[128,2048]{1,0:T(8,128)(2,1)} %lf_hbm.1, bf16[128,2048]{1,0:T(8,128)(2,1)} %rf_hbm.1, f32[64,2048]{1,0:T(8,128)} %lp_hbm.1, f32[64,2048]{1,0:T(8,128)} %rp_hbm.1, f32[1,64]{1,0:T(1,128)} %bitcast.6, f32[16,128]{1,0:T(8,128)} %bitcast.4, ...), custom_call_target="tpu_custom_call" | custom-call | tf_op jit(solution)/shard_map/pallas_call | solution.py:273
  81.1 0.0 copy-start
  81.1 1.9 %copy.13 = f32[64,2048]{1,0:T(8,128)} copy(f32[64,2048]{1,0:T(8,128)} %get-tuple-element.12) | data formatting | bytes 1048576
  83.1 0.0 copy-done
  83.1 0.0 copy-start.1
  83.1 0.8 copy.14
  83.9 0.0 copy-done.1
  83.9 0.5 copy.15
Async XLA Ops:
  81.1 1.9 %copy-start = (f32[64,2048]{1,0:T(8,128)S(1)}, f32[64,2048]{1,0:T(8,128)}, u32[]{:S(2)}) copy-start(f32[64,2048]{1,0:T(8,128)} %get-tuple-element.13) | copy-start | bytes 1572868
  83.1 0.8 copy-start.1

commit v2 on v1

--- a/solution.py
+++ b/solution.py
@@ -27,12 +27,12 @@
     li_ref,
     lm_ref,
     rm_ref,
-    ol_hbm,
-    or_hbm,
+    plan,
+    rs,
+    scale_ref,
     oi_ref,
     lf,
     rf,
-    plan,
     grad,
     src,
     r1,
@@ -41,11 +41,8 @@
     m1,
     m2,
     rx,
-    rs,
     c1,
-    c2,
     load_sem,
-    store_sem,
     send_sem,
     recv_sem,
 ):
@@ -55,10 +52,17 @@
     tiles = points // LANES
     rank = half * nx
     y, z, c, x = (lax.axis_index(a) for a in ("y", "z", "c", "x"))
-    yc_size, zx_size = ny * nc, nz * nx
-    yc, zx = y * nc + c, z * nx + x
+    yc_size, zx_size, row_size = ny * nc, nz * nx, ny * nz * nc
+    yc, zx, row = y * nc + c, z * nx + x, (y * nz + z) * nc + c
     piece = LANES // yc_size
 
+    row_peers = [
+        {"y": lax.rem(y + dy, ny), "z": lax.rem(z + dz, nz), "c": lax.rem(c + dc, nc)}
+        for dy in far_first(ny) + [0]
+        for dz in far_first(nz) + [0]
+        for dc in range(nc)
+        if dy or dz or dc
+    ]
     yc_peers = [
         {"y": lax.rem(y + dy, ny), "c": lax.rem(c + dc, nc)}
         for dy in far_first(ny) + [0]
@@ -88,7 +92,7 @@
     for load in loads:
         load.start()
     barrier = pltpu.get_barrier_semaphore()
-    greeted = zx_peers + yc_peers
+    greeted = yc_peers + z_peers + x_peers
     for peer in greeted:
         pl.semaphore_signal(
             barrier, inc=1, device_id=peer, device_id_type=pl.DeviceIdType.MESH
@@ -228,32 +232,34 @@
             for t in range(tiles):
                 acc += plan[rows, t * LANES : (t + 1) * LANES] * rs[side, t : t + 1, :]
             sums.append(jnp.sum(acc, axis=1, keepdims=True))
-        c1[turn, yc] = to_row(jnp.concatenate(sums, axis=0))
-        spread(stage + 2, c1.at[turn, yc], yc_peers)
-        arrived(stage + 2, c1.at[turn, pl.ds(0, yc_size - 1)])
-        c2[turn, z] = jnp.sum(c1[turn], axis=0)
-        spread(stage + 3, c2.at[turn, z], z_peers)
-        arrived(stage + 3, c2.at[turn, pl.ds(0, nz - 1)])
-        totals = jnp.sum(c2[turn], axis=0)
+        c1[turn, row] = to_row(jnp.concatenate(sums, axis=0))
+        spread(stage + 2, c1.at[turn, row], row_peers)
+        arrived(stage + 2, c1.at[turn, pl.ds(0, row_size - 1)])
+        totals = jnp.sum(c1[turn], axis=0)
         mixed = jnp.log(scale_row * totals)
         log_inner = (log_inner + (mixed + swap(mixed))) / 3.0
         scale_row = jnp.exp(log_inner) / totals
         scale = to_column(scale_row)
-        stage += 4
+        stage += 3
 
     oi_ref[...] = (log_inner - jnp.log(mean_left))[:, :half]
+    scale_ref[...] = jnp.broadcast_to(scale, (LANES, LANES))
+    for number, bulk in sent:
+        pltpu.make_async_copy(bulk, bulk, send_sem.at[number]).wait()
+
+
+def finish(tilted, rs, scale, oi_in, ol_hbm, or_hbm, oi_out, out, store_sem):
+    half = LANES // 2
+    oi_out[...] = oi_in[...]
     stores = []
-    for side, rows, _ in sides:
-        for t in range(tiles):
+    for side, target in ((0, ol_hbm), (1, or_hbm)):
+        rows = slice(side * half, (side + 1) * half)
+        for t in range(rs.shape[1]):
             at = slice(t * LANES, (t + 1) * LANES)
-            grad[rows, at] = rs[side, t : t + 1, :] * plan[rows, at] * scale[rows]
-        store = pltpu.make_async_copy(
-            grad.at[rows], (ol_hbm, or_hbm)[side], store_sem.at[side]
-        )
+            out[rows, at] = rs[side, t : t + 1, :] * tilted[rows, at] * scale[rows, :]
+        store = pltpu.make_async_copy(out.at[rows], target, store_sem.at[side])
         store.start()
         stores.append(store)
-    for number, bulk in sent:
-        pltpu.make_async_copy(bulk, bulk, send_sem.at[number]).wait()
     for store in stores:
         store.wait()
 
@@ -267,22 +273,23 @@
     tiles = points // LANES
     yc_size, zx_size = ny * nc, nz * nx
     piece = LANES // yc_size
-    stages = 5 + 4 * ITERS
-    hbm = pl.BlockSpec(memory_space=pl.ANY)
+    row_size = ny * nz * nc
+    stages = 5 + 3 * ITERS
+    hbm = pl.BlockSpec(memory_space=pltpu.HBM)
     vmem = pl.BlockSpec(memory_space=pltpu.VMEM)
-    new_left, new_right, new_log_inner = pl.pallas_call(
+    tilted, row_scale, col_scale, new_log_inner = pl.pallas_call(
         functools.partial(kernel, sizes),
         out_shape=(
-            jax.ShapeDtypeStruct((columns, points), F32),
-            jax.ShapeDtypeStruct((columns, points), F32),
-            jax.ShapeDtypeStruct((1, columns), F32),
+            pltpu.VMEM((2 * columns, points), F32),
+            pltpu.VMEM((2, tiles, LANES), F32),
+            pltpu.VMEM((LANES, LANES), F32),
+            pltpu.VMEM((1, columns), F32),
         ),
         in_specs=[hbm] * 4 + [vmem] * 3,
-        out_specs=(hbm, hbm, vmem),
+        out_specs=(vmem, vmem, vmem, vmem),
         scratch_shapes=[
             pltpu.VMEM((depth, points), jnp.bfloat16),
             pltpu.VMEM((depth, points), jnp.bfloat16),
-            pltpu.VMEM((2 * columns, points), F32),
             pltpu.VMEM((2 * columns, points), F32),
             pltpu.VMEM((yc_size, piece + 1, LANES), F32),
             pltpu.VMEM((yc_size, piece + 1, LANES), F32),
@@ -291,15 +298,14 @@
             pltpu.VMEM((yc_size, 1, LANES), F32),
             pltpu.VMEM((zx_size, 1, LANES), F32),
             pltpu.VMEM((ITERS, 2, nx, tiles, LANES), F32),
-            pltpu.VMEM((2, tiles, LANES), F32),
-            pltpu.VMEM((ITERS, yc_size, 1, LANES), F32),
-            pltpu.VMEM((ITERS, nz, 1, LANES), F32),
+            pltpu.VMEM((ITERS, row_size, 1, LANES), F32),
             pltpu.SemaphoreType.DMA((4,)),
-            pltpu.SemaphoreType.DMA((2,)),
             pltpu.SemaphoreType.DMA((stages,)),
             pltpu.SemaphoreType.DMA((stages,)),
         ],
-        compiler_params=pltpu.CompilerParams(collective_id=0, has_side_effects=True),
+        compiler_params=pltpu.CompilerParams(
+            collective_id=0, has_side_effects=True, vmem_limit_bytes=60 << 20
+        ),
     )(
         left_factor,
         right_factor,
@@ -308,6 +314,26 @@
         log_inner.reshape(1, columns),
         left_mass.reshape(tiles, LANES),
         right_mass.reshape(tiles, LANES),
+    )
+    new_left, new_right, new_log_inner = pl.pallas_call(
+        finish,
+        out_shape=(
+            jax.ShapeDtypeStruct((columns, points), F32),
+            jax.ShapeDtypeStruct((columns, points), F32),
+            jax.ShapeDtypeStruct((1, columns), F32),
+        ),
+        in_specs=[vmem] * 4,
+        out_specs=(hbm, hbm, vmem),
+        scratch_shapes=[
+            pltpu.VMEM((2 * columns, points), F32),
+            pltpu.SemaphoreType.DMA((2,)),
+        ],
+        compiler_params=pltpu.CompilerParams(vmem_limit_bytes=8 << 20),
+    )(
+        *(
+            pltpu.with_memory_space_constraint(value, pltpu.VMEM)
+            for value in (tilted, row_scale, col_scale, new_log_inner)
+        )
     )
     return new_left, new_right, new_log_inner.reshape(columns)
 

time: 84.6 us -> 75.8 us (0.90)
  Pallas kernels: 80.5 us -> 75 us
  local copies, waits for them, and re-layouts: 3.24 us -> 0 us
    pallas_call x1 -> x2, Pallas kernels: 80.5 us -> 75 us  [the longest x1 73.5 us: per_device(): pl.pallas_call(functools.partial(kernel, sizes), out_shape=(pltpu.VMEM((2...]
    unnamed x7 -> x0, local copies, waits for them, and re-layouts: 3.24 us -> none
where the time goes in v2:
time: 75.8 us; the launch traced here: 75.7 us
  Pallas kernels  75 us (99%)
    pallas_call x1, Pallas kernels, per_device(): pl.pallas_call(functools.partial(kernel, sizes), out_shape=(pltpu.VMEM((2...  73.5 us
    pallas_call x1, Pallas kernels, per_device(): pl.pallas_call(finish, out_shape=(jax.ShapeDtypeStruct((columns, points),...  1.54 us

profile of v2, /device:TPU:1, one launch (start us, length us, event | category | flops | bytes accessed | tf_op | source)
XLA Modules:
  0.0 75.7 jit_solution(2067186573413877591)
XLA Ops:
  0.6 73.5 %shard_map.94 = (f32[128,2048]{1,0:T(8,128)S(1)}, f32[2,16,128]{2,1,0:T(8,128)S(1)}, f32[128,128]{1,0:T(8,128)S(1)}, f32[1,64]{1,0:T(1,128)S(1)}) custom-call(bf16[128,2048]{1,0:T(8,128)(2,1)} %lf_hbm.1, bf16[128,2048]{1,0:T(8,128)(2,1)} %rf_hbm.1, f32[64,2048]{1,0:T(8,128)} %lp_hbm.1, f32[64,2048]{1,0:T(8,128)} %rp_hbm.1, f32[1,64]{1,0:T(1,128)} %bitcast.6, ...), custom_call_target="tpu_custom_call" | custom-call | tf_op jit(solution)/shard_map/pallas_call | solution.py:280
  74.1 1.5 %shard_map.95 = (f32[64,2048]{1,0:T(8,128)}, f32[64,2048]{1,0:T(8,128)}, f32[1,64]{1,0:T(1,128)}) custom-call(f32[128,2048]{1,0:T(8,128)S(1)} %get-tuple-element.10.tilted, f32[2,16,128]{2,1,0:T(8,128)S(1)} %get-tuple-element.11.rs, f32[128,128]{1,0:T(8,128)S(1)} %get-tuple-element.12.scale, f32[1,64]{1,0:T(1,128)S(1)} %get-tuple-element.13.oi_in), custom_call_target="tpu_custom_call" | custom-call | tf_op jit(solution)/shard_map/pallas_call | solution.py:318
